TPU v7x, 32 devices: a whole 2x2x4 slice. The times are simulated.
32 devices in a mesh: band: 8 (over z, y), ga: 4 (over x, core).
Axes of the slice: x: 2, y: 2, z: 4, core: 2. Of those that a mesh axis runs over, the one named last changes fastest.
Arguments:
- orbitals: float32 [8, 96, 9216], P('band', 'ga'), may hold values from -6 to 6
- retained: int32 [96, 9216], P(None, 'ga'), may hold values 0 or 1
Outputs:
- exchange_field: float32 [8, 96, 9216], P('band', 'ga')
- block_matrix: float32 [8, 1], P('band')
All inputs are finite; a program needn't handle non-finite values. No bound on the sum of `retained` on one device may be relied on, other than what follows from the above.
Results may differ from a plain program's by a relative error of at most 0.0086.
Values may be sent and summed in bfloat16 or wider, within the bound.
A program may use at most 64 MiB of HBM per device.

v0:
```python
import functools
import math

import jax
import jax.numpy as jnp
import numpy as np
from jax import lax
from jax.experimental import pallas as pl
from jax.experimental.pallas import tpu as pltpu
from jax.sharding import PartitionSpec as P

MESH = pl.DeviceIdType.MESH
LANES = 128


def cas_numpy(length):
    counter = np.arange(length)
    product = (counter[:, None] * counter[None, :] % length).astype(np.float32)
    angles = np.float32(2.0 * np.pi / length) * product
    return (np.cos(angles) + np.sin(angles)) / np.sqrt(np.float32(length))


def tables(length):
    pack = math.lcm(length, LANES) // length
    tiles = pack * length // LANES
    cas = cas_numpy(length)
    order = np.arange(length).reshape(length // pack, pack).T.reshape(-1)
    second = cas[order][:, order]
    spread = np.zeros((pack * LANES, pack * length), np.float32)
    for q in range(pack):
        spread[q * LANES : q * LANES + length, q * length : (q + 1) * length] = cas
    forward = np.stack(
        [spread[t * LANES : (t + 2) * LANES, t * LANES : (t + 1) * LANES] for t in range(tiles)]
    )
    backward = np.stack(
        [
            spread[0 : 2 * LANES, 0 : 2 * LANES].T,
            spread[2 * LANES : 4 * LANES, LANES : 3 * LANES].T,
        ]
    )
    as_bf16 = lambda v: jnp.asarray(v, jnp.bfloat16)
    return as_bf16(cas), as_bf16(second), as_bf16(forward), as_bf16(backward)


def wrapped_numpy(length):
    k = np.arange(length)
    return np.where(k < length // 2, k, k - length).astype(np.float32)


def split_lanes(tile_list):
    t0, t1, t2 = tile_list
    lane = lax.broadcasted_iota(jnp.int32, t0.shape, 1)
    roll = lambda v, s: pltpu.roll(v, s, 1)
    z1 = jnp.where(lane < 32, roll(t0, 32), roll(t1, 32))
    z2 = jnp.where(lane < 64, roll(t1, 64), roll(t2, 64))
    return [t0, z1, z2, roll(t2, 96)]


def join_lanes(z):
    lane = lax.broadcasted_iota(jnp.int32, z[0].shape, 1)
    roll = lambda v, s: pltpu.roll(v, s, 1)
    r1, r2, r3 = roll(z[1], 96), roll(z[2], 64), roll(z[3], 32)
    return [
        jnp.where(lane < 96, z[0], r1),
        jnp.where(lane < 64, r1, r2),
        jnp.where(lane < 32, r2, r3),
    ]


def dot(a, b):
    return jnp.dot(a, b, preferred_element_type=jnp.float32)


def exchange_kernel(
    length, groups, bands, give_back,
    phi_hbm, kept_hbm, plane_hbm, cas_hbm, second_hbm, fwd_hbm, bwd_hbm,
    out_hbm, extra_ref,
    out_ref, phi_ref, kept_ref, plane_ref, cas_ref, second_ref, fwd_ref, bwd_ref, own, guest, running, turn, screen, phi_out, phi_in,
    spec_out, spec_in, pot_out, pot_in, part_out, part_in, joined, sums,
    load_sem, out_sem, band_send, band_recv, fwd_send, fwd_recv, bwd_send, bwd_recv, sum_send, sum_recv,
):
    slab = length // groups
    pack = 4
    wide = pack * length
    blocks = length // pack
    dev_blocks = blocks // groups
    step = 8
    chunks = slab // step
    chunk_rows = blocks * step
    dev_rows = dev_blocks * step
    tiles = wide // LANES
    me = lax.axis_index("ga")
    band = lax.axis_index("band")
    upper = lax.rem(band + 1, bands)
    lower = lax.rem(band + bands - 1, bands)
    half = groups // 2
    chip, core = me // 2, me % 2
    offsets = [(dx, dc) for dx in range(half - 1, -1, -1) for dc in range(2) if (dx, dc) != (0, 0)]
    peers = [((chip + dx) % half) * 2 + (core + dc) % 2 for dx, dc in offsets]

    loads = [
        pltpu.make_async_copy(
            phi_hbm.at[pl.ds(c * step, step)], phi_ref.at[pl.ds(c * step, step)], load_sem.at[c]
        )
        for c in range(chunks)
    ]
    for src, dst in (
        (second_hbm, second_ref), (fwd_hbm, fwd_ref), (cas_hbm, cas_ref), (bwd_hbm, bwd_ref),
        (plane_hbm, plane_ref), (kept_hbm, kept_ref),
    ):
        loads.append(pltpu.make_async_copy(src, dst, load_sem.at[len(loads)]))
    for load in loads:
        load.start()
    barrier = pltpu.get_barrier_semaphore()
    for peer in peers:
        pl.semaphore_signal(barrier, inc=1, device_id=(band, peer), device_id_type=MESH)
    for other in (upper, lower):
        pl.semaphore_signal(barrier, inc=1, device_id=(other, me), device_id_type=MESH)
    started = []

    def send(src, dst, send_sem, recv_sem, target):
        copy = pltpu.make_async_remote_copy(
            src, dst, send_sem, recv_sem, device_id=target, device_id_type=MESH
        )
        copy.start()
        started.append(copy)
        return copy

    def tiles_of(value):
        return [value[:, t * LANES : (t + 1) * LANES] for t in range(tiles)]

    def strided(c, i):
        return pl.ds(c * chunk_rows + i, blocks, stride=step)

    def planes(buf, c, i):
        return jnp.concatenate([turn[buf, q, strided(c, i), :] for q in range(pack)], axis=0)

    def put(buf, c, i, plane):
        for q in range(pack):
            turn[buf, q, strided(c, i), :] = plane[q * blocks : (q + 1) * blocks]

    def block_rows(c, b):
        return slice(c * chunk_rows + b * step, c * chunk_rows + (b + 2) * step)

    def unjoin(buf, c, b, both):
        for q, z in enumerate(split_lanes(tiles_of(both))):
            turn[buf, q, block_rows(c, b), :] = z

    def join(buf, c, b, target):
        found = join_lanes([turn[buf, q, block_rows(c, b), :] for q in range(pack)])
        for t, tile in enumerate(found):
            target[block_rows(c, b), t * LANES : (t + 1) * LANES] = tile.astype(target.dtype)

    def rows_of(ref, c):
        return ref.at[pl.ds(c * chunk_rows, chunk_rows)]

    phi_copies = []
    for c in range(chunks):
        loads[c].wait()
        for b in range(0, blocks, 2):
            both = jnp.concatenate(
                [
                    phi_ref[c * step : (c + 1) * step, (b + i) * wide : (b + i + 1) * wide]
                    for i in range(2)
                ],
                axis=0,
            )
            phi_out[block_rows(c, b), :] = both.astype(jnp.bfloat16)
            unjoin(0, c, b, both)
        if c == 0:
            pl.semaphore_wait(barrier, len(peers) + 2)
        phi_copies.append(
            send(rows_of(phi_out, c), rows_of(phi_in, c), band_send.at[0, c], band_recv.at[0, c], (upper, me))
        )
        for i in range(step):
            own[c * step + i] = planes(0, c, i)

    def forward(pair, c, left, right, buf):
        for i in range(0, step, 2):
            rho = jnp.concatenate(
                [
                    (left[c * step + i + j] * right[c * step + i + j]).astype(jnp.bfloat16)
                    for j in range(2)
                ],
                axis=1,
            )
            res = dot(second_ref[...], rho)
            for j in range(2):
                put(buf, c, i + j, res[:, j * LANES : (j + 1) * LANES])
        z = [
            turn[buf, q, c * chunk_rows : (c + 1) * chunk_rows, :].astype(jnp.bfloat16)
            for q in range(pack)
        ]
        for t in range(tiles):
            res = dot(jnp.concatenate([z[t], z[t + 1]], axis=1), fwd_ref[t]).astype(jnp.bfloat16)
            for g in range(groups):
                spec_out[pair, c, g, :, t * LANES : (t + 1) * LANES] = res[
                    g * dev_rows : (g + 1) * dev_rows
                ]
        copies = [
            send(
                spec_out.at[pair, c, peer], spec_in.at[pair, c, me],
                fwd_send.at[pair, c, k], fwd_recv.at[pair, c, k], (band, peer),
            )
            for k, peer in enumerate(peers)
        ]
        spec_in[pair, c, me] = spec_out[pair, c, me]
        return copies

    def middle(pair, copies):
        for copy in copies:
            copy.wait_recv()
        for b in range(0, dev_blocks, 2):
            lo, hi = b * step, (b + 2) * step
            parts = [
                spec_in[pair, c, s, lo:hi, :].astype(jnp.float32)
                for s in range(groups)
                for c in range(chunks)
            ]
            rhs = jnp.concatenate(
                [
                    jnp.concatenate([p[i * step : (i + 1) * step] for p in parts], axis=0)
                    for i in range(2)
                ],
                axis=1,
            ).astype(jnp.bfloat16)
            spectrum = dot(cas_ref[...], rhs)
            weighted = (spectrum * screen[:, b * wide : (b + 2) * wide]).astype(jnp.bfloat16)
            back = dot(cas_ref[...], weighted)
            for s in range(groups):
                for c in range(chunks):
                    piece = back[s * slab + c * step : s * slab + (c + 1) * step]
                    pot_out[pair, c, s, lo:hi, :] = jnp.concatenate(
                        [piece[:, :wide], piece[:, wide:]], axis=0
                    ).astype(jnp.bfloat16)

    def send_back(pair, c):
        copies = [
            send(
                pot_out.at[pair, c, peer], pot_in.at[pair, c, me],
                bwd_send.at[pair, c, k], bwd_recv.at[pair, c, k], (band, peer),
            )
            for k, peer in enumerate(peers)
        ]
        pot_in[pair, c, me] = pot_out[pair, c, me]
        return copies

    def backward(pair, c, copies, buf, use):
        for copy in copies:
            copy.wait_recv()
        value = pot_in[pair, c].reshape(chunk_rows, wide)
        for h in range(2):
            res = dot(value[:, h * LANES : (h + 2) * LANES], bwd_ref[h])
            for i in range(2):
                turn[buf, 2 * h + i, c * chunk_rows : (c + 1) * chunk_rows, :] = res[
                    :, i * LANES : (i + 1) * LANES
                ]
        for i in range(0, step, 2):
            two = jnp.concatenate([planes(buf, c, i), planes(buf, c, i + 1)], axis=1)
            res = dot(second_ref[...], two.astype(jnp.bfloat16))
            for j in range(2):
                use(c, i + j, res[:, j * LANES : (j + 1) * LANES])

    for load in loads[chunks : chunks + 4]:
        load.wait()
    first = [copy for c in range(chunks) for copy in forward(0, c, own, own, 1)]

    for load in loads[chunks + 4 :]:
        load.wait()
    freq = lax.broadcasted_iota(jnp.int32, (length, 1), 0)
    freq = jnp.where(freq < length // 2, freq, freq - length).astype(jnp.float32)
    scale = 1.0 / ((length / 4.0) * (length / 4.0))
    for c in range(0, dev_blocks):
        cols = slice(c * wide, (c + 1) * wide)
        squared = freq * freq + plane_ref[me, :, cols]
        screen[:, cols] = kept_ref[:, cols].astype(jnp.float32) / (1.0 + squared * scale)

    def guest_forward(c):
        phi_copies[c].wait_recv()
        for b in range(0, blocks, 2):
            unjoin(2, c, b, phi_in[block_rows(c, b), :].astype(jnp.float32))
        for i in range(step):
            guest[c * step + i] = planes(2, c, i)
        return forward(1, c, own, guest, 1)

    def use_first(c, i, field):
        put(2, c, i, running[c * step + i] + field * own[c * step + i])

    def use_second(c, i, field):
        x = c * step + i
        put(1, c, i, field * own[x])
        running[x] = field * guest[x]

    second = []
    for c in range(chunks):
        second += guest_forward(c)
    middle(0, first)
    middle(1, second)
    second_back = [send_back(1, c) for c in range(chunks)]
    first_back = [send_back(0, c) for c in range(chunks)]
    part_copies = []
    for c in range(chunks):
        backward(1, c, second_back[c], 0, use_second)
        for b in range(0, blocks, 2):
            join(1, c, b, part_out)
        if give_back:
            part_copies.append(
                send(rows_of(part_out, c), rows_of(part_in, c), band_send.at[1, c], band_recv.at[1, c], (lower, me))
            )
    for c in range(chunks):
        backward(0, c, first_back[c], 0, use_first)
    for c in range(chunks):
        for b in range(0, blocks, 2):
            join(2, c, b, joined)
    total = jnp.zeros((step, LANES), jnp.float32)
    outs = []
    for c in range(chunks):
        if give_back:
            part_copies[c].wait_recv()
        for b in range(0, blocks, 2):
            value = joined[block_rows(c, b), :]
            if give_back:
                value = value + part_in[block_rows(c, b), :].astype(jnp.float32)
            for i in range(2):
                piece = value[i * step : (i + 1) * step]
                here = (slice(c * step, (c + 1) * step), slice((b + i) * wide, (b + i + 1) * wide))
                out_ref[here] = piece
                if give_back:
                    for tile in tiles_of(piece * phi_ref[here]):
                        total = total + tile
        rows = pl.ds(c * step, step)
        outs.append(pltpu.make_async_copy(out_ref.at[rows], out_hbm.at[rows], out_sem.at[c]))
        outs[c].start()
    if give_back:
        sums[me] = total
        sum_copies = [
            send(sums.at[me], sums.at[me], sum_send.at[k], sum_recv.at[k], (band, peer))
            for k, peer in enumerate(peers)
        ]
        for copy in sum_copies:
            copy.wait_recv()
        whole = sums[0]
        for s in range(1, groups):
            whole = whole + sums[s]
        whole = jnp.sum(jnp.sum(whole, axis=0, keepdims=True), axis=1, keepdims=True)
        extra_ref[...] = whole * (1.0 / float(length**3))
    else:
        extra_ref[...] = part_out[...]
    for copy in started:
        copy.wait_send()
    for copy in outs:
        copy.wait()


def fused(orbitals, retained, groups, bands, give_back):
    length = retained.shape[0]
    slab = length // groups
    pack = math.lcm(length, LANES) // length
    assert pack == 4 and orbitals.shape[0] == 1
    wide = pack * length
    blocks = length // pack
    rows = blocks * slab
    squares = wrapped_numpy(length) ** 2
    plane = (squares[:, None] + squares[None, :]).reshape(groups, 1, -1).astype(np.float32)
    plane = np.broadcast_to(plane, (groups, 1, plane.shape[2]))
    cas, second, fwd, bwd = tables(length)
    bf16, f32 = jnp.bfloat16, jnp.float32
    chunks = slab // 8
    exchange = lambda: pltpu.VMEM((2, chunks, groups, rows // groups // chunks, wide), bf16)
    merged = lambda kind: pltpu.VMEM((rows, wide), kind)
    cube = lambda: pltpu.VMEM((slab, length, LANES), f32)
    dma = pltpu.SemaphoreType.DMA
    extra = (
        jax.ShapeDtypeStruct((1, 1), f32) if give_back else jax.ShapeDtypeStruct((rows, wide), bf16)
    )
    vmem = pl.BlockSpec(memory_space=pltpu.VMEM)
    return pl.pallas_call(
        functools.partial(exchange_kernel, length, groups, bands, give_back),
        out_shape=(jax.ShapeDtypeStruct((slab, length * length), f32), extra),
        in_specs=[pl.BlockSpec(memory_space=pltpu.HBM)] * 7,
        out_specs=(pl.BlockSpec(memory_space=pltpu.HBM), vmem),
        scratch_shapes=[
            pltpu.VMEM((slab, length * length), f32),
            pltpu.VMEM((slab, length * length), f32),
            pltpu.VMEM(retained.shape, jnp.int32),
            pltpu.VMEM(plane.shape, f32),
            *[pltpu.VMEM(v.shape, bf16) for v in (cas, second, fwd, bwd)],
            cube(), cube(), cube(),
            pltpu.VMEM((3, pack, rows, LANES), f32),
            pltpu.VMEM((length, length * length // groups), f32),
            merged(bf16), merged(bf16),
            exchange(), exchange(), exchange(), exchange(),
            merged(bf16), merged(bf16), merged(f32),
            pltpu.VMEM((groups, 8, LANES), f32),
            dma((chunks + 6,)), dma((chunks,)),
            dma((2, chunks)), dma((2, chunks)),
            *[dma((2, chunks, groups)) for _ in range(4)],
            dma((groups,)), dma((groups,)),
        ],
        compiler_params=pltpu.CompilerParams(
            collective_id=0, has_side_effects=True, vmem_limit_bytes=62914560
        ),
    )(orbitals[0], retained, jnp.asarray(plane), cas, second, fwd, bwd)


def passed_along(value, axis, steps):
    count = lax.axis_size(axis)
    pairs = [(source, (source + steps) % count) for source in range(count)]
    return lax.ppermute(value, axis, pairs)


def transform_axis(density, table, form):
    return jnp.einsum(form, density, table, preferred_element_type=jnp.float32).astype(jnp.bfloat16)


def later_rounds(orbitals, retained, running, carried, band_reach):
    bands_dev, slab_rows, plane_cells = orbitals.shape
    length = retained.shape[0]
    groups = lax.axis_size("ga")
    column_rows = length // groups
    lattice = orbitals.reshape(bands_dev, slab_rows, length, length)
    table = jnp.asarray(cas_numpy(length), jnp.bfloat16)
    squares = jnp.asarray(wrapped_numpy(length) ** 2)
    local_y = lax.dynamic_slice_in_dim(squares, lax.axis_index("ga") * column_rows, column_rows)
    squared = squares[:, None, None] + local_y[None, :, None] + squares[None, None, :]
    spread = length / 4.0
    screen = retained.reshape(length, column_rows, length).astype(jnp.float32) / (
        1.0 + squared / (spread * spread)
    )

    def potentials(density):
        spectrum = transform_axis(density, table, "pxyz,kz->pxyk")
        spectrum = transform_axis(spectrum, table, "pxyz,ky->pxkz")
        spectrum = lax.all_to_all(spectrum, "ga", split_axis=2, concat_axis=1, tiled=True)
        spectrum = transform_axis(spectrum, table, "pxyz,kx->pkyz")
        spectrum = (spectrum.astype(jnp.float32) * screen).astype(jnp.bfloat16)
        spectrum = transform_axis(spectrum, table, "pxyz,kx->pkyz")
        spectrum = lax.all_to_all(spectrum, "ga", split_axis=1, concat_axis=2, tiled=True)
        spectrum = transform_axis(spectrum, table, "pxyz,ky->pxkz")
        return transform_axis(spectrum, table, "pxyz,kz->pxyk").astype(jnp.float32)

    def round_once(_, state):
        visiting, partial_field, running_sum = state
        visiting = passed_along(visiting, "band", 1)
        partial_field = passed_along(partial_field.astype(jnp.bfloat16), "band", 1)
        guests = visiting.astype(jnp.float32)
        fields = potentials((lattice * guests).astype(jnp.bfloat16))
        return (
            visiting,
            partial_field.astype(jnp.float32) + fields * lattice,
            running_sum + fields * guests,
        )

    visitors = passed_along(lattice.astype(jnp.bfloat16), "band", 1)
    _, carried, running = lax.fori_loop(
        1, band_reach, round_once,
        (visitors, carried.reshape(lattice.shape), running.reshape(lattice.shape)),
    )
    running = running + passed_along(
        carried.astype(jnp.bfloat16), "band", -band_reach
    ).astype(jnp.float32)
    flat, flat_running = lattice.reshape(bands_dev, -1), running.reshape(bands_dev, -1)
    block = jnp.dot(flat, flat_running.T, precision=lax.Precision.HIGHEST)
    return running.reshape(orbitals.shape), lax.psum(block, "ga") / float(length**3)


def local(orbitals, retained):
    groups, bands = lax.axis_size("ga"), lax.axis_size("band")
    band_reach = max(1, bands // 8)
    running, extra = fused(orbitals, retained, groups, bands, band_reach == 1)
    if band_reach == 1:
        return running[None], extra
    slab = orbitals.shape[1]
    wide = extra.shape[1]
    carried = extra.reshape(slab // 8, -1, 8, wide).transpose(0, 2, 1, 3).astype(jnp.float32)
    return later_rounds(orbitals, retained, running[None], carried.reshape(orbitals.shape), band_reach)


def solution(mesh):
    placed = (P("band", "ga", None), P(None, "ga"))
    return jax.shard_map(
        local,
        mesh=mesh,
        in_specs=placed,
        out_specs=(P("band", "ga", None), P("band", None)),
        check_vma=False,
    )
```

profile of v0, /device:TPU:0, one launch (start us, length us, event | category | flops | bytes accessed | tf_op | source)
XLA Modules:
  0.0 46.6 jit_solution(8254734791937171711)
XLA Ops:
  0.6 42.0 %shard_map.86 = (f32[24,9216]{1,0:T(8,128)}, f32[1,1]{1,0:T(1,128)}) custom-call(f32[24,9216]{1,0:T(8,128)} %bitcast.2, s32[96,2304]{1,0:T(8,128)} %kept_hbm.1, f32[4,1,2304]{2,1,0:T(1,128)} %constant.14.clone.plane_hbm, bf16[96,96]{1,0:T(8,128)(2,1)} %constant.10.clone.cas_hbm, bf16[96,96]{1,0:T(8,128)(2,1)} %constant.11.clone.second_hbm, ...), custom_call_target="tpu_custom_call" | custom-call | tf_op jit(solution)/shard_map/pallas_call | solution.py:377
  42.6 2.1 %copy.11 = f32[1,24,9216]{2,1,0:T(8,128)} copy(f32[1,24,9216]{2,1,0:T(8,128)} %bitcast.3) | data formatting | bytes 1769472
where the time goes:
time: 46.8 us; the launch traced here: 46.6 us
  Pallas kernels  42 us (90%)
  between operations  2.44 us (5%)
  local copies, waits for them, and re-layouts  2.14 us (5%)
    pallas_call x1, Pallas kernels, fused(): pl.pallas_call(functools.partial(exchange_kernel, length, groups, bands,...  42 us
    unnamed x1, local copies, waits for them, and re-layouts  2.14 us

commit v1 on v0

--- a/solution.py
+++ b/solution.py
@@ -74,10 +74,10 @@
 def exchange_kernel(
     length, groups, bands, give_back,
     phi_hbm, kept_hbm, plane_hbm, cas_hbm, second_hbm, fwd_hbm, bwd_hbm,
-    out_hbm, extra_ref,
-    out_ref, phi_ref, kept_ref, plane_ref, cas_ref, second_ref, fwd_ref, bwd_ref, own, guest, running, turn, screen, phi_out, phi_in,
-    spec_out, spec_in, pot_out, pot_in, part_out, part_in, joined, sums,
-    load_sem, out_sem, band_send, band_recv, fwd_send, fwd_recv, bwd_send, bwd_recv, sum_send, sum_recv,
+    out_ref, extra_ref,
+    phi_ref, kept_ref, plane_ref, cas_ref, second_ref, fwd_ref, bwd_ref, own, guest, running, turn, screen, phi_out, phi_in,
+    spec_out, spec_in, pot_out, pot_in, part_out, part_in, joined, sums, passed,
+    load_sem, phi_sent, phi_got, fwd_sent, fwd_got, bwd_sent, bwd_got, part_sent, part_got, sum_sent, sum_got, pass_sent, pass_got,
 ):
     slab = length // groups
     pack = 4
@@ -114,20 +114,24 @@
     barrier = pltpu.get_barrier_semaphore()
     for peer in peers:
         pl.semaphore_signal(barrier, inc=1, device_id=(band, peer), device_id_type=MESH)
-    for other in (upper, lower):
-        pl.semaphore_signal(barrier, inc=1, device_id=(other, me), device_id_type=MESH)
-    started = []
+    pl.semaphore_signal(barrier, inc=1, device_id=(lower, me), device_id_type=MESH)
 
     def send(src, dst, send_sem, recv_sem, target):
         copy = pltpu.make_async_remote_copy(
             src, dst, send_sem, recv_sem, device_id=target, device_id_type=MESH
         )
         copy.start()
-        started.append(copy)
         return copy
 
-    def tiles_of(value):
-        return [value[:, t * LANES : (t + 1) * LANES] for t in range(tiles)]
+    def all_of(src, dst, send_sem, recv_sem):
+        return pltpu.make_async_remote_copy(
+            src, dst, send_sem, recv_sem, device_id=(upper, me), device_id_type=MESH
+        )
+
+    def split_tiles(value):
+        return [value[:, t : t + LANES] for t in range(0, value.shape[1], LANES)]
+
+    tiles_of = split_tiles
 
     def strided(c, i):
         return pl.ds(c * chunk_rows + i, blocks, stride=step)
@@ -168,9 +172,9 @@
             phi_out[block_rows(c, b), :] = both.astype(jnp.bfloat16)
             unjoin(0, c, b, both)
         if c == 0:
-            pl.semaphore_wait(barrier, len(peers) + 2)
+            pl.semaphore_wait(barrier, len(peers) + 1)
         phi_copies.append(
-            send(rows_of(phi_out, c), rows_of(phi_in, c), band_send.at[0, c], band_recv.at[0, c], (upper, me))
+            send(rows_of(phi_out, c), rows_of(phi_in, c), phi_sent, phi_got.at[c], (upper, me))
         )
         for i in range(step):
             own[c * step + i] = planes(0, c, i)
@@ -197,19 +201,16 @@
                 spec_out[pair, c, g, :, t * LANES : (t + 1) * LANES] = res[
                     g * dev_rows : (g + 1) * dev_rows
                 ]
-        copies = [
-            send(
-                spec_out.at[pair, c, peer], spec_in.at[pair, c, me],
-                fwd_send.at[pair, c, k], fwd_recv.at[pair, c, k], (band, peer),
-            )
-            for k, peer in enumerate(peers)
-        ]
+        for peer in peers:
+            send(spec_out.at[pair, c, peer], spec_in.at[pair, c, me], fwd_sent, fwd_got.at[pair], (band, peer))
         spec_in[pair, c, me] = spec_out[pair, c, me]
-        return copies
-
-    def middle(pair, copies):
-        for copy in copies:
-            copy.wait_recv()
+
+    others = pl.ds(0, groups - 1)
+
+    def middle(pair):
+        arrived = spec_in.at[pair, :, others]
+        all_of(arrived, arrived, fwd_sent, fwd_got.at[pair]).wait_recv()
+        energy = jnp.zeros((step, LANES), jnp.float32)
         for b in range(0, dev_blocks, 2):
             lo, hi = b * step, (b + 2) * step
             parts = [
@@ -225,29 +226,27 @@
                 axis=1,
             ).astype(jnp.bfloat16)
             spectrum = dot(cas_ref[...], rhs)
-            weighted = (spectrum * screen[:, b * wide : (b + 2) * wide]).astype(jnp.bfloat16)
-            back = dot(cas_ref[...], weighted)
+            weighted = spectrum * screen[:, b * wide : (b + 2) * wide]
+            for r in range(0, length, step):
+                for tile in split_tiles(spectrum[r : r + step] * weighted[r : r + step]):
+                    energy = energy + tile
+            back = dot(cas_ref[...], weighted.astype(jnp.bfloat16))
             for s in range(groups):
                 for c in range(chunks):
                     piece = back[s * slab + c * step : s * slab + (c + 1) * step]
                     pot_out[pair, c, s, lo:hi, :] = jnp.concatenate(
                         [piece[:, :wide], piece[:, wide:]], axis=0
                     ).astype(jnp.bfloat16)
+        return energy
 
     def send_back(pair, c):
-        copies = [
-            send(
-                pot_out.at[pair, c, peer], pot_in.at[pair, c, me],
-                bwd_send.at[pair, c, k], bwd_recv.at[pair, c, k], (band, peer),
-            )
-            for k, peer in enumerate(peers)
-        ]
+        for peer in peers:
+            send(pot_out.at[pair, c, peer], pot_in.at[pair, c, me], bwd_sent, bwd_got.at[pair, c], (band, peer))
         pot_in[pair, c, me] = pot_out[pair, c, me]
-        return copies
-
-    def backward(pair, c, copies, buf, use):
-        for copy in copies:
-            copy.wait_recv()
+
+    def backward(pair, c, buf, use):
+        arrived = pot_in.at[pair, c, others]
+        all_of(arrived, arrived, bwd_sent, bwd_got.at[pair, c]).wait_recv()
         value = pot_in[pair, c].reshape(chunk_rows, wide)
         for h in range(2):
             res = dot(value[:, h * LANES : (h + 2) * LANES], bwd_ref[h])
@@ -263,7 +262,8 @@
 
     for load in loads[chunks : chunks + 4]:
         load.wait()
-    first = [copy for c in range(chunks) for copy in forward(0, c, own, own, 1)]
+    for c in range(chunks):
+        forward(0, c, own, own, 1)
 
     for load in loads[chunks + 4 :]:
         load.wait()
@@ -281,7 +281,7 @@
             unjoin(2, c, b, phi_in[block_rows(c, b), :].astype(jnp.float32))
         for i in range(step):
             guest[c * step + i] = planes(2, c, i)
-        return forward(1, c, own, guest, 1)
+        forward(1, c, own, guest, 1)
 
     def use_first(c, i, field):
         put(2, c, i, running[c * step + i] + field * own[c * step + i])
@@ -291,29 +291,47 @@
         put(1, c, i, field * own[x])
         running[x] = field * guest[x]
 
-    second = []
-    for c in range(chunks):
-        second += guest_forward(c)
-    middle(0, first)
-    middle(1, second)
-    second_back = [send_back(1, c) for c in range(chunks)]
-    first_back = [send_back(0, c) for c in range(chunks)]
+    for c in range(chunks):
+        guest_forward(c)
+    energy = middle(0)
+    shared = middle(1)
+    for c in range(chunks):
+        send_back(1, c)
+    if give_back:
+        passed[0] = shared
+        pass_copy = send(passed.at[0], passed.at[1], pass_sent, pass_got, (lower, me))
+        sums[me] = energy + shared
+    for c in range(chunks):
+        send_back(0, c)
     part_copies = []
     for c in range(chunks):
-        backward(1, c, second_back[c], 0, use_second)
+        backward(1, c, 0, use_second)
         for b in range(0, blocks, 2):
             join(1, c, b, part_out)
         if give_back:
             part_copies.append(
-                send(rows_of(part_out, c), rows_of(part_in, c), band_send.at[1, c], band_recv.at[1, c], (lower, me))
+                send(rows_of(part_out, c), rows_of(part_in, c), part_sent, part_got.at[c], (lower, me))
             )
-    for c in range(chunks):
-        backward(0, c, first_back[c], 0, use_first)
+    if give_back:
+        pass_copy.wait_recv()
+        sums[me] = sums[me] + passed[1]
+        for peer in peers:
+            send(sums.at[me], sums.at[me], sum_sent, sum_got, (band, peer))
+    for c in range(chunks):
+        backward(0, c, 0, use_first)
     for c in range(chunks):
         for b in range(0, blocks, 2):
             join(2, c, b, joined)
-    total = jnp.zeros((step, LANES), jnp.float32)
-    outs = []
+    if give_back:
+        arrived = sums.at[others]
+        all_of(arrived, arrived, sum_sent, sum_got).wait_recv()
+        whole = sums[0]
+        for s in range(1, groups):
+            whole = whole + sums[s]
+        whole = jnp.sum(jnp.sum(whole, axis=0, keepdims=True), axis=1, keepdims=True)
+        extra_ref[...] = whole * (1.0 / float(length**3))
+    else:
+        extra_ref[...] = part_out[...]
     for c in range(chunks):
         if give_back:
             part_copies[c].wait_recv()
@@ -322,34 +340,18 @@
             if give_back:
                 value = value + part_in[block_rows(c, b), :].astype(jnp.float32)
             for i in range(2):
-                piece = value[i * step : (i + 1) * step]
-                here = (slice(c * step, (c + 1) * step), slice((b + i) * wide, (b + i + 1) * wide))
-                out_ref[here] = piece
-                if give_back:
-                    for tile in tiles_of(piece * phi_ref[here]):
-                        total = total + tile
-        rows = pl.ds(c * step, step)
-        outs.append(pltpu.make_async_copy(out_ref.at[rows], out_hbm.at[rows], out_sem.at[c]))
-        outs[c].start()
+                here = (0, slice(c * step, (c + 1) * step), slice((b + i) * wide, (b + i + 1) * wide))
+                out_ref[here] = value[i * step : (i + 1) * step]
+    all_of(phi_out, phi_in, phi_sent, phi_got.at[0]).wait_send()
+    leaving = spec_out.at[:, :, others]
+    all_of(leaving, leaving, fwd_sent, fwd_got.at[0]).wait_send()
+    leaving = pot_out.at[:, :, others]
+    all_of(leaving, leaving, bwd_sent, bwd_got.at[0, 0]).wait_send()
     if give_back:
-        sums[me] = total
-        sum_copies = [
-            send(sums.at[me], sums.at[me], sum_send.at[k], sum_recv.at[k], (band, peer))
-            for k, peer in enumerate(peers)
-        ]
-        for copy in sum_copies:
-            copy.wait_recv()
-        whole = sums[0]
-        for s in range(1, groups):
-            whole = whole + sums[s]
-        whole = jnp.sum(jnp.sum(whole, axis=0, keepdims=True), axis=1, keepdims=True)
-        extra_ref[...] = whole * (1.0 / float(length**3))
-    else:
-        extra_ref[...] = part_out[...]
-    for copy in started:
-        copy.wait_send()
-    for copy in outs:
-        copy.wait()
+        pass_copy.wait_send()
+        leaving = sums.at[others]
+        all_of(leaving, leaving, sum_sent, sum_got).wait_send()
+        all_of(part_out, part_in, part_sent, part_got.at[0]).wait_send()
 
 
 def fused(orbitals, retained, groups, bands, give_back):
@@ -376,11 +378,10 @@
     vmem = pl.BlockSpec(memory_space=pltpu.VMEM)
     return pl.pallas_call(
         functools.partial(exchange_kernel, length, groups, bands, give_back),
-        out_shape=(jax.ShapeDtypeStruct((slab, length * length), f32), extra),
+        out_shape=(pltpu.VMEM((1, slab, length * length), f32), extra),
         in_specs=[pl.BlockSpec(memory_space=pltpu.HBM)] * 7,
-        out_specs=(pl.BlockSpec(memory_space=pltpu.HBM), vmem),
+        out_specs=(vmem, vmem),
         scratch_shapes=[
-            pltpu.VMEM((slab, length * length), f32),
             pltpu.VMEM((slab, length * length), f32),
             pltpu.VMEM(retained.shape, jnp.int32),
             pltpu.VMEM(plane.shape, f32),
@@ -391,11 +392,10 @@
             merged(bf16), merged(bf16),
             exchange(), exchange(), exchange(), exchange(),
             merged(bf16), merged(bf16), merged(f32),
-            pltpu.VMEM((groups, 8, LANES), f32),
-            dma((chunks + 6,)), dma((chunks,)),
-            dma((2, chunks)), dma((2, chunks)),
-            *[dma((2, chunks, groups)) for _ in range(4)],
-            dma((groups,)), dma((groups,)),
+            pltpu.VMEM((groups, 8, LANES), f32), pltpu.VMEM((2, 8, LANES), f32),
+            dma((chunks + 6,)), dma, dma((chunks,)),
+            dma, dma((2,)), dma, dma((2, chunks)),
+            *([dma, dma((chunks,)), dma, dma, dma, dma] if give_back else [dma] * 6),
         ],
         compiler_params=pltpu.CompilerParams(
             collective_id=0, has_side_effects=True, vmem_limit_bytes=62914560
@@ -469,11 +469,11 @@
     band_reach = max(1, bands // 8)
     running, extra = fused(orbitals, retained, groups, bands, band_reach == 1)
     if band_reach == 1:
-        return running[None], extra
+        return running, extra
     slab = orbitals.shape[1]
     wide = extra.shape[1]
     carried = extra.reshape(slab // 8, -1, 8, wide).transpose(0, 2, 1, 3).astype(jnp.float32)
-    return later_rounds(orbitals, retained, running[None], carried.reshape(orbitals.shape), band_reach)
+    return later_rounds(orbitals, retained, running, carried.reshape(orbitals.shape), band_reach)
 
 
 def solution(mesh):

time: 46.8 us -> 40.7 us (0.87)
  Pallas kernels: 42 us -> 37.3 us
  local copies, waits for them, and re-layouts: 2.14 us -> 0.91 us
    pallas_call x1, Pallas kernels: 42 us -> 37.3 us  [fused(): pl.pallas_call(functools.partial(exchange_kernel, length, groups, bands,...]
    unnamed x1, local copies, waits for them, and re-layouts: 2.14 us -> 0.91 us
where the time goes in v1:
time: 40.7 us; the launch traced here: 40.5 us
  Pallas kernels  37.3 us (92%)
  between operations  2.33 us (6%)
  local copies, waits for them, and re-layouts  0.91 us (2%)
    pallas_call x1, Pallas kernels, fused(): pl.pallas_call(functools.partial(exchange_kernel, length, groups, bands,...  37.3 us
    unnamed x1, local copies, waits for them, and re-layouts  0.91 us

profile of v1, /device:TPU:0, one launch (start us, length us, event | category | flops | bytes accessed | tf_op | source)
XLA Modules:
  0.0 40.5 jit_solution(10696013267838949814)
XLA Ops:
  0.6 37.3 %shard_map.86 = (f32[1,24,9216]{2,1,0:T(8,128)S(1)}, f32[1,1]{1,0:T(1,128)}) custom-call(f32[24,9216]{1,0:T(8,128)} %bitcast.1, s32[96,2304]{1,0:T(8,128)} %kept_hbm.1, f32[4,1,2304]{2,1,0:T(1,128)} %constant.14.clone.plane_hbm, bf16[96,96]{1,0:T(8,128)(2,1)} %constant.10.clone.cas_hbm, bf16[96,96]{1,0:T(8,128)(2,1)} %constant.11.clone.second_hbm, ...), custom_call_target="tpu_custom_call" | custom-call | tf_op jit(solution)/shard_map/pallas_call | solution.py:379
  37.9 0.9 %copy.11 = f32[1,24,9216]{2,1,0:T(8,128)} copy(f32[1,24,9216]{2,1,0:T(8,128)S(1)} %get-tuple-element.2) | data formatting | bytes 1769472
